TPU v7x, 32 devices: a whole 2x2x4 slice. The times are simulated.
32 devices in a mesh: lat: 2 (over core), lon: 2 (over y), lev: 2 (over x), unit: 4 (over z).
Axes of the slice: x: 2, y: 2, z: 4, core: 2. Of those that a mesh axis runs over, the one named last changes fastest.
Arguments:
- tracer: float32 [32, 256, 32, 128], P(('unit', 'lat'), 'lon', 'lev'), parts along dimension 0, may hold values from 0.5 to 2
- diffusivity: float32 [32, 256, 32, 128], P(('unit', 'lat'), 'lon', 'lev'), parts along dimension 0, may hold values from 0.03 to 0.15
- source: float32 [32, 256, 32, 128], P(('unit', 'lat'), 'lon', 'lev'), parts along dimension 0, may hold values from -0.2 to 0.2
Outputs:
- standardized: float32 [32, 256, 32, 128], P(('unit', 'lat'), 'lon', 'lev'), parts along dimension 0
- tracer_end: float32 [32, 256, 32, 128], P(('unit', 'lat'), 'lon', 'lev'), parts along dimension 0
There are 4 independent parts, one for each index of `unit`. A program takes and returns all parts, laid end to end along the dimension named above; each array names one. Nothing has to cross between parts.
All inputs are finite; a program needn't handle non-finite values.
Results may differ from a plain program's by a relative error of at most 0.00002.
Values sent between devices are 32-bit elements; how exact they have to be, the bound alone decides.
A program may use at most 128 MiB of HBM per device.

v0:
```python
import jax
import jax.numpy as jnp
from jax import lax
from jax.sharding import PartitionSpec as P

STEPS = 4


def extended(block, sides, width):
    for axis, dim in sides:
        count = lax.axis_size(axis)
        forward = [(i, i + 1) for i in range(count - 1)]
        forward.append((count - 1, 0))
        backward = [(target, source) for source, target in forward]
        low = lax.ppermute(
            lax.slice_in_dim(block, block.shape[dim] - width, None, axis=dim), axis, forward
        )
        high = lax.ppermute(lax.slice_in_dim(block, 0, width, axis=dim), axis, backward)
        block = jnp.concatenate([low, block, high], axis=dim)
    return block


def strip_edges(values, dims):
    for dim in dims:
        values = lax.slice_in_dim(values, 1, values.shape[dim] - 1, axis=dim)
    return values


def neighbour(values, dim, start, dims):
    others = [other for other in dims if other != dim]
    values = strip_edges(values, others)
    return lax.slice_in_dim(values, start, start + values.shape[dim] - 2, axis=dim)


def one_step(padded, diffusivity, source):
    middle = strip_edges(padded, (0, 1, 2))
    lower = [neighbour(padded, dim, 0, (0, 1, 2)) for dim in (0, 1, 2)]
    upper = [neighbour(padded, dim, 2, (0, 1, 2)) for dim in (0, 1, 2)]
    spread = lower[0] + upper[0] + lower[1] + upper[1] + lower[2] + upper[2] - 6.0 * middle
    return middle + diffusivity * spread + source


def on_device(tracer, diffusivity, source):
    for step in range(STEPS):
        padded = extended(tracer, (("lat", 0), ("lon", 1), ("lev", 2)), 1)
        tracer = one_step(padded, diffusivity, source)
    count = tracer.shape[2] * lax.axis_size("lev")
    guess = 1.0
    moved = tracer - guess
    totals, squares = lax.psum(
        (jnp.sum(moved, axis=2, keepdims=True), jnp.sum(moved * moved, axis=2, keepdims=True)),
        "lev",
    )
    line_mean = guess + totals / count
    centred = tracer - line_mean
    line_variance = squares / count - totals / count * (totals / count)
    standardized = centred * lax.rsqrt(line_variance + 0.0001)
    return (standardized, tracer)


def solution(mesh):
    return jax.shard_map(
        on_device,
        mesh=mesh,
        in_specs=(
            P(("unit", "lat"), "lon", "lev", None),
            P(("unit", "lat"), "lon", "lev", None),
            P(("unit", "lat"), "lon", "lev", None),
        ),
        out_specs=(P(("unit", "lat"), "lon", "lev", None), P(("unit", "lat"), "lon", "lev", None)),
        check_vma=False,
    )
```

profile of v0, /device:TPU:0, one launch (start us, length us, event | category | flops | bytes accessed | tf_op | source)
XLA Modules:
  0.0 216.6 jit_solution(12756258185716158385)
XLA Ops:
  7.2 3.5 %copy.12 = f32[4,128,16,128]{3,1,2,0:T(8,128)S(1)} copy(f32[4,128,16,128]{3,2,1,0:T(8,128)} %param.3) | data formatting | bytes 8388608 | tf_op args[0]
  10.7 0.2 fusion.41
  10.9 0.6 collective-permute-start
  11.5 0.1 collective-permute-start.1
  11.6 1.3 copy-done.3
  12.8 1.0 collective-permute-done
  13.8 0.1 constant_dynamic-update-slice_fusion.2
  13.9 0.5 copy-done.4
  14.4 1.3 constant_dynamic-update-slice_fusion.1
  15.7 0.1 constant_dynamic-update-slice_fusion
  15.9 3.1 %collective-permute-start.2 = (f32[6,1,16,128]{3,1,2,0:T(1,128)S(1)}, f32[6,1,16,128]{3,1,2,0:T(1,128)S(1)}, u32[]{:S(2)}, u32[]{:S(2)}) collective-permute-start(f32[6,1,16,128]{3,1,2,0:T(1,128)S(1)} %get-tuple-element.23), channel_id=1, source_target_pairs={{0,8},{8,0},{1,9},{9,1},{2,10},{10,2},{3,11},{11,3},{4,12},{12,4},... | collective-permute-start | bytes 147464 | tf_op jit(solution)/shard_map/ppermute | solution.py:15
  19.0 0.1 collective-permute-start.3
  19.0 2.0 collective-permute-done.2
  21.0 2.0 collective-permute-done.3
  23.1 1.6 collective-permute-start.4
  24.7 0.5 collective-permute-start.5
  25.2 10.5 %collective-permute-done.4 = f32[6,130,1,128]{3,1,2,0:T(8,128)S(1)} collective-permute-done((f32[6,130,1,128]{3,1,2,0:T(8,128)S(1)}, f32[6,130,1,128]{3,1,2,0:T(8,128)S(1)}, u32[]{:S(2)}, u32[]{:S(2)}) %collective-permute-start.4) | collective-permute-done | bytes 399392 | tf_op jit(solution)/shard_map/ppermute | solution.py:15
  35.7 6.7 %collective-permute-done.5 = f32[6,130,1,128]{3,1,2,0:T(8,128)S(1)} collective-permute-done((f32[6,130,1,128]{3,1,2,0:T(8,128)S(1)}, f32[6,130,1,128]{3,1,2,0:T(8,128)S(1)}, u32[]{:S(2)}, u32[]{:S(2)}) %collective-permute-start.5) | collective-permute-done | bytes 399392 | tf_op jit(solution)/shard_map/ppermute | solution.py:18
  42.5 14.5 %fusion.31 = f32[4,128,16,128]{3,1,2,0:T(8,128)S(1)} fusion(f32[4,128,16,128]{3,1,2,0:T(8,128)} %copy-done.3, f32[6,130,1,128]{3,1,2,0:T(8,128)S(1)} %collective-permute-done.5, f32[6,1,16,128]{3,1,2,0:T(1,128)S(1)} %collective-permute-done.3, f32[6,128,16,128]{3,1,2,0:T(8,128)} %copy-done.2, f32[6,1,16,128]{3,1,2,0:T(1,128)S(1)} %collective-permute-done.2, ...), kind=kLoop, calls=%fused_computation.86 | loop fusion | flops 20971520 | bytes 26062848 | tf_op jit(solution)/shard_map/add | solution.py:40
  56.9 0.1 fusion.40
  57.2 0.5 collective-permute-start.7
  57.7 2.1 collective-permute-done.6
  59.8 1.5 collective-permute-done.7
  61.4 0.5 collective-permute-start.8
  61.9 1.6 collective-permute-start.9
  63.5 2.3 %collective-permute-done.8 = f32[6,1,16,128]{3,1,2,0:T(1,128)S(1)} collective-permute-done((f32[6,1,16,128]{3,1,2,0:T(1,128)S(1)}, f32[6,1,16,128]{3,1,2,0:T(1,128)S(1)}, u32[]{:S(2)}, u32[]{:S(2)}) %collective-permute-start.8) | collective-permute-done | bytes 49184 | tf_op jit(solution)/shard_map/ppermute | solution.py:15
  65.8 0.5 collective-permute-done.9
  66.3 0.1 pad_maximum_fusion.78
  66.4 1.8 collective-permute-start.10
  68.2 0.3 collective-permute-start.11
  68.5 10.5 %collective-permute-done.10 = f32[6,130,1,128]{3,1,2,0:T(8,128)S(1)} collective-permute-done((f32[6,130,1,128]{3,1,2,0:T(8,128)S(1)}, f32[6,130,1,128]{3,1,2,0:T(8,128)S(1)}, u32[]{:S(2)}, u32[]{:S(2)}) %collective-permute-start.10) | collective-permute-done | bytes 399392 | tf_op jit(solution)/shard_map/ppermute | solution.py:15
  78.9 7.3 %collective-permute-done.11 = f32[6,130,1,128]{3,1,2,0:T(8,128)S(1)} collective-permute-done((f32[6,130,1,128]{3,1,2,0:T(8,128)S(1)}, f32[6,130,1,128]{3,1,2,0:T(8,128)S(1)}, u32[]{:S(2)}, u32[]{:S(2)}) %collective-permute-start.11) | collective-permute-done | bytes 399392 | tf_op jit(solution)/shard_map/ppermute | solution.py:18
  86.2 7.9 %fusion.22 = f32[4,128,16,128]{3,1,2,0:T(8,128)S(1)} fusion(f32[4,128,16,128]{3,1,2,0:T(8,128)S(1)} %fusion.31, f32[6,130,1,128]{3,1,2,0:T(8,128)S(1)} %collective-permute-done.11, f32[6,1,16,128]{3,1,2,0:T(1,128)S(1)} %collective-permute-done.9, f32[6,1,16,128]{3,1,2,0:T(1,128)S(1)} %collective-permute-done.8, ...), kind=kLoop, calls=%fused_computation.59 | loop fusion | flops 29360128 | bytes 19771392 | tf_op jit(solution)/shard_map/add | solution.py:40
  94.2 0.2 fusion.39
  94.5 0.5 collective-permute-start.13
  95.0 2.1 collective-permute-done.12
  97.1 1.5 collective-permute-done.13
  98.7 0.8 collective-permute-start.14
  99.5 1.3 collective-permute-start.15
  100.8 2.3 %collective-permute-done.14 = f32[6,1,16,128]{3,1,2,0:T(1,128)S(1)} collective-permute-done((f32[6,1,16,128]{3,1,2,0:T(1,128)S(1)}, f32[6,1,16,128]{3,1,2,0:T(1,128)S(1)}, u32[]{:S(2)}, u32[]{:S(2)}) %collective-permute-start.14) | collective-permute-done | bytes 49184 | tf_op jit(solution)/shard_map/ppermute | solution.py:15
  103.0 0.5 collective-permute-done.15
  103.7 1.8 collective-permute-start.16
  105.5 0.3 collective-permute-start.17
  105.8 10.5 %collective-permute-done.16 = f32[6,130,1,128]{3,1,2,0:T(8,128)S(1)} collective-permute-done((f32[6,130,1,128]{3,1,2,0:T(8,128)S(1)}, f32[6,130,1,128]{3,1,2,0:T(8,128)S(1)}, u32[]{:S(2)}, u32[]{:S(2)}) %collective-permute-start.16) | collective-permute-done | bytes 399392 | tf_op jit(solution)/shard_map/ppermute | solution.py:15
  116.2 7.2 %collective-permute-done.17 = f32[6,130,1,128]{3,1,2,0:T(8,128)S(1)} collective-permute-done((f32[6,130,1,128]{3,1,2,0:T(8,128)S(1)}, f32[6,130,1,128]{3,1,2,0:T(8,128)S(1)}, u32[]{:S(2)}, u32[]{:S(2)}) %collective-permute-start.17) | collective-permute-done | bytes 399392 | tf_op jit(solution)/shard_map/ppermute | solution.py:18
  123.5 8.0 %fusion.13 = f32[4,128,16,128]{3,1,2,0:T(8,128)S(1)} fusion(f32[4,128,16,128]{3,1,2,0:T(8,128)S(1)} %fusion.22, f32[6,130,1,128]{3,1,2,0:T(8,128)S(1)} %collective-permute-done.17, f32[6,1,16,128]{3,1,2,0:T(1,128)S(1)} %collective-permute-done.15, f32[6,1,16,128]{3,1,2,0:T(1,128)S(1)} %collective-permute-done.14, ...), kind=kLoop, calls=%fused_computation.32 | loop fusion | flops 29360128 | bytes 19771392 | tf_op jit(solution)/shard_map/add | solution.py:40
  131.5 0.2 fusion.38
  131.8 0.5 collective-permute-start.19
  132.3 2.1 collective-permute-done.18
  134.4 1.5 collective-permute-done.19
  136.0 1.3 collective-permute-start.20
  137.3 0.8 collective-permute-start.21
  138.1 2.5 %collective-permute-done.20 = f32[6,1,16,128]{3,1,2,0:T(1,128)S(1)} collective-permute-done((f32[6,1,16,128]{3,1,2,0:T(1,128)S(1)}, f32[6,1,16,128]{3,1,2,0:T(1,128)S(1)}, u32[]{:S(2)}, u32[]{:S(2)}) %collective-permute-start.20) | collective-permute-done | bytes 49184 | tf_op jit(solution)/shard_map/ppermute | solution.py:15
  140.6 0.8 collective-permute-done.21
  141.5 1.7 collective-permute-start.22
  143.2 0.4 collective-permute-start.23
  143.6 10.5 %collective-permute-done.22 = f32[6,130,1,128]{3,1,2,0:T(8,128)S(1)} collective-permute-done((f32[6,130,1,128]{3,1,2,0:T(8,128)S(1)}, f32[6,130,1,128]{3,1,2,0:T(8,128)S(1)}, u32[]{:S(2)}, u32[]{:S(2)}) %collective-permute-start.22) | collective-permute-done | bytes 399392 | tf_op jit(solution)/shard_map/ppermute | solution.py:15
  154.0 7.4 %collective-permute-done.23 = f32[6,130,1,128]{3,1,2,0:T(8,128)S(1)} collective-permute-done((f32[6,130,1,128]{3,1,2,0:T(8,128)S(1)}, f32[6,130,1,128]{3,1,2,0:T(8,128)S(1)}, u32[]{:S(2)}, u32[]{:S(2)}) %collective-permute-start.23) | collective-permute-done | bytes 399392 | tf_op jit(solution)/shard_map/ppermute | solution.py:18
  161.4 10.2 %add_reduce_fusion = (f32[4,128,128]{2,1,0:T(8,128)}, f32[4,128,128]{2,1,0:T(8,128)}, f32[4,128,16,128]{3,1,2,0:T(8,128)}) fusion(f32[4,128,16,128]{3,2,1,0:T(8,128)S(1)} %copy-done, f32[4,128,16,128]{3,1,2,0:T(8,128)S(1)} %fusion.13, f32[6,130,1,128]{3,1,2,0:T(8,128)S(1)} %collective-permute-done.23, f32[6,1,16,128]{3,1,2,0:T(1,128)S(1)} %collective-permute-done.21, ...), kind=kLoop, calls=%fused_computation.102 | loop fusion | flops 33423360 | bytes 20295680 | tf_op jit(solution)/shard_map/reduce_sum | solution.py:51
  171.7 6.6 %copy.21 = f32[4,128,16,128]{3,2,1,0:T(8,128)} copy(f32[4,128,16,128]{3,1,2,0:T(8,128)} %get-tuple-element.8) | data formatting | bytes 8388608
  178.3 22.9 %all-reduce.3.cloned.1.call-done = (f32[4,128,1,128]{3,1,0,2:T(8,128)}, f32[4,128,1,128]{3,1,0,2:T(8,128)}) async-done(((f32[4,128,1,128]{3,1,0,2:T(8,128)}, f32[4,128,1,128]{3,1,0,2:T(8,128)}), (f32[4,128,1,128]{3,1,0,2:T(8,128)}, f32[4,128,1,128]{3,1,0,2:T(8,128)})) %all-reduce.3.cloned.1.call-update) | async-done | bytes 524304 | tf_op jit(solution)/shard_map/psum | solution.py:50
  201.2 1.1 add_bitcast_fusion
  202.3 3.0 %subtract_multiply_fusion = f32[4,128,16,128]{3,1,2,0:T(8,128)S(1)} fusion(f32[4,128,16,128]{3,1,2,0:T(8,128)} %get-tuple-element.8, f32[4,128,128]{2,1,0:T(8,128)S(1)} %get-tuple-element.34, f32[4,128,128]{2,1,0:T(8,128)S(1)} %get-tuple-element.33), kind=kLoop, calls=%fused_computation.101 | loop fusion | flops 2097152 | bytes 8912896 | tf_op jit(solution)/shard_map/mul | solution.py:57
  205.3 4.4 %copy.20 = f32[4,128,16,128]{3,2,1,0:T(8,128)} copy(f32[4,128,16,128]{3,1,2,0:T(8,128)S(1)} %subtract_multiply_fusion) | data formatting | bytes 8388608
  (21 shorter events, 0.8 us)
Async XLA Ops:
  7.2 194.0 %all-reduce.3.cloned.1.call-start = ((), (), s32[]{:S(2)}) async-start(), calls=%async_computation | async-start | bytes 1048576 | tf_op jit(solution)/shard_map/psum | solution.py:50
  10.7 2.1 copy-start.3
  10.7 3.7 %copy-start.4 = (f32[4,128,16,128]{3,2,1,0:T(8,128)S(1)}, f32[4,128,16,128]{3,2,1,0:T(8,128)}, u32[]{:S(2)}) copy-start(f32[4,128,16,128]{3,2,1,0:T(8,128)} %param.3) | copy-start | bytes 12582916
  10.9 2.8 %collective-permute-start = (f32[1,128,16,128]{3,1,2,0:T(8,128)S(1)}, f32[1,128,16,128]{3,1,2,0:T(8,128)S(1)}, u32[]{:S(2)}, u32[]{:S(2)}) collective-permute-start(f32[1,128,16,128]{3,1,2,0:T(8,128)S(1)} %get-tuple-element.32), channel_id=1, source_target_pairs={{0,16},{16,0},{1,17},{17,1},{2,18},{18,2},{3,19},{19,3},{4,20},{20... | collective-permute-start | bytes 3145736 | tf_op jit(solution)/shard_map/ppermute | solution.py:15
  11.5 4.2 %collective-permute-start.1 = (f32[1,128,16,128]{3,1,2,0:T(8,128)S(1)}, f32[1,128,16,128]{3,1,2,0:T(8,128)S(1)}, u32[]{:S(2)}, u32[]{:S(2)}) collective-permute-start(f32[1,128,16,128]{3,1,2,0:T(8,128)S(1)} %get-tuple-element.31), channel_id=1, source_target_pairs={{16,0},{0,16},{17,1},{1,17},{18,2},{2,18},{19,3},{3,19},{20,4},{4,... | collective-permute-start | bytes 3145736 | tf_op jit(solution)/shard_map/ppermute | solution.py:18
  15.8 19.9 %copy-start.2 = (f32[6,128,16,128]{3,1,2,0:T(8,128)}, f32[6,128,16,128]{3,1,2,0:T(8,128)S(1)}, u32[]{:S(2)}) copy-start(f32[6,128,16,128]{3,1,2,0:T(8,128)S(1)} %constant_dynamic-update-slice_fusion) | copy-start | bytes 18874372
  15.8 26.6 %copy-start = (f32[4,128,16,128]{3,2,1,0:T(8,128)S(1)}, f32[4,128,16,128]{3,2,1,0:T(8,128)}, u32[]{:S(2)}) copy-start(f32[4,128,16,128]{3,2,1,0:T(8,128)} %param.5) | copy-start | bytes 12582916
  15.9 5.1 %collective-permute-start.2 = (f32[6,1,16,128]{3,1,2,0:T(1,128)S(1)}, f32[6,1,16,128]{3,1,2,0:T(1,128)S(1)}, u32[]{:S(2)}, u32[]{:S(2)}) collective-permute-start(f32[6,1,16,128]{3,1,2,0:T(1,128)S(1)} %get-tuple-element.23), channel_id=1, source_target_pairs={{0,8},{8,0},{1,9},{9,1},{2,10},{10,2},{3,11},{11,3},{4,12},{12,4},... | collective-permute-start | bytes 147464 | tf_op jit(solution)/shard_map/ppermute | solution.py:15
  19.0 4.1 %collective-permute-start.3 = (f32[6,1,16,128]{3,1,2,0:T(1,128)S(1)}, f32[6,1,16,128]{3,1,2,0:T(1,128)S(1)}, u32[]{:S(2)}, u32[]{:S(2)}) collective-permute-start(f32[6,1,16,128]{3,1,2,0:T(1,128)S(1)} %get-tuple-element.24), channel_id=1, source_target_pairs={{8,0},{0,8},{9,1},{1,9},{10,2},{2,10},{11,3},{3,11},{12,4},{4,12},... | collective-permute-start | bytes 147464 | tf_op jit(solution)/shard_map/ppermute | solution.py:18
  23.1 12.6 %collective-permute-start.4 = (f32[6,130,1,128]{3,1,2,0:T(8,128)S(1)}, f32[6,130,1,128]{3,1,2,0:T(8,128)S(1)}, u32[]{:S(2)}, u32[]{:S(2)}) collective-permute-start(f32[6,130,1,128]{3,1,2,0:T(8,128)S(1)} %get-tuple-element.15), channel_id=1, source_target_pairs={{0,4},{4,0},{1,5},{5,1},{2,6},{6,2},{3,7},{7,3},{8,12},{12,8},{9,1... | collective-permute-start | bytes 1198088 | tf_op jit(solution)/shard_map/ppermute | solution.py:15
  24.7 17.8 %collective-permute-start.5 = (f32[6,130,1,128]{3,1,2,0:T(8,128)S(1)}, f32[6,130,1,128]{3,1,2,0:T(8,128)S(1)}, u32[]{:S(2)}, u32[]{:S(2)}) collective-permute-start(f32[6,130,1,128]{3,1,2,0:T(8,128)S(1)} %get-tuple-element.16), channel_id=1, source_target_pairs={{4,0},{0,4},{5,1},{1,5},{6,2},{2,6},{7,3},{3,7},{12,8},{8,12},{13,... | collective-permute-start | bytes 1198088 | tf_op jit(solution)/shard_map/ppermute | solution.py:18
  57.1 2.7 %collective-permute-start.6 = (f32[1,128,16,128]{3,1,2,0:T(8,128)S(1)}, f32[1,128,16,128]{3,1,2,0:T(8,128)S(1)}, u32[]{:S(2)}, u32[]{:S(2)}) collective-permute-start(f32[1,128,16,128]{3,1,2,0:T(8,128)S(1)} %get-tuple-element.29), channel_id=1, source_target_pairs={{0,16},{16,0},{1,17},{17,1},{2,18},{18,2},{3,19},{19,3},{4,20},{20... | collective-permute-start | bytes 3145736 | tf_op jit(solution)/shard_map/ppermute | solution.py:15
  57.2 4.1 %collective-permute-start.7 = (f32[1,128,16,128]{3,1,2,0:T(8,128)S(1)}, f32[1,128,16,128]{3,1,2,0:T(8,128)S(1)}, u32[]{:S(2)}, u32[]{:S(2)}) collective-permute-start(f32[1,128,16,128]{3,1,2,0:T(8,128)S(1)} %get-tuple-element.30), channel_id=1, source_target_pairs={{16,0},{0,16},{17,1},{1,17},{18,2},{2,18},{19,3},{3,19},{20,4},{4,... | collective-permute-start | bytes 3145736 | tf_op jit(solution)/shard_map/ppermute | solution.py:18
  61.4 24.8 %copy-start.1 = (f32[4,128,16,128]{3,2,1,0:T(8,128)S(1)}, f32[4,128,16,128]{3,2,1,0:T(8,128)}, u32[]{:S(2)}) copy-start(f32[4,128,16,128]{3,2,1,0:T(8,128)} %param.4) | copy-start | bytes 12582916
  61.4 4.4 %collective-permute-start.8 = (f32[6,1,16,128]{3,1,2,0:T(1,128)S(1)}, f32[6,1,16,128]{3,1,2,0:T(1,128)S(1)}, u32[]{:S(2)}, u32[]{:S(2)}) collective-permute-start(f32[6,1,16,128]{3,1,2,0:T(1,128)S(1)} %get-tuple-element.21), channel_id=1, source_target_pairs={{0,8},{8,0},{1,9},{9,1},{2,10},{10,2},{3,11},{11,3},{4,12},{12,4},... | collective-permute-start | bytes 147464 | tf_op jit(solution)/shard_map/ppermute | solution.py:15
  61.9 4.4 %collective-permute-start.9 = (f32[6,1,16,128]{3,1,2,0:T(1,128)S(1)}, f32[6,1,16,128]{3,1,2,0:T(1,128)S(1)}, u32[]{:S(2)}, u32[]{:S(2)}) collective-permute-start(f32[6,1,16,128]{3,1,2,0:T(1,128)S(1)} %get-tuple-element.22), channel_id=1, source_target_pairs={{8,0},{0,8},{9,1},{1,9},{10,2},{2,10},{11,3},{3,11},{12,4},{4,12},... | collective-permute-start | bytes 147464 | tf_op jit(solution)/shard_map/ppermute | solution.py:18
  66.4 12.6 %collective-permute-start.10 = (f32[6,130,1,128]{3,1,2,0:T(8,128)S(1)}, f32[6,130,1,128]{3,1,2,0:T(8,128)S(1)}, u32[]{:S(2)}, u32[]{:S(2)}) collective-permute-start(f32[6,130,1,128]{3,1,2,0:T(8,128)S(1)} %get-tuple-element.13), channel_id=1, source_target_pairs={{0,4},{4,0},{1,5},{5,1},{2,6},{6,2},{3,7},{7,3},{8,12},{12,8},{9,1... | collective-permute-start | bytes 1198088 | tf_op jit(solution)/shard_map/ppermute | solution.py:15
  68.2 18.0 %collective-permute-start.11 = (f32[6,130,1,128]{3,1,2,0:T(8,128)S(1)}, f32[6,130,1,128]{3,1,2,0:T(8,128)S(1)}, u32[]{:S(2)}, u32[]{:S(2)}) collective-permute-start(f32[6,130,1,128]{3,1,2,0:T(8,128)S(1)} %get-tuple-element.14), channel_id=1, source_target_pairs={{4,0},{0,4},{5,1},{1,5},{6,2},{2,6},{7,3},{3,7},{12,8},{8,12},{13,... | collective-permute-start | bytes 1198088 | tf_op jit(solution)/shard_map/ppermute | solution.py:18
  94.4 2.7 %collective-permute-start.12 = (f32[1,128,16,128]{3,1,2,0:T(8,128)S(1)}, f32[1,128,16,128]{3,1,2,0:T(8,128)S(1)}, u32[]{:S(2)}, u32[]{:S(2)}) collective-permute-start(f32[1,128,16,128]{3,1,2,0:T(8,128)S(1)} %get-tuple-element.27), channel_id=1, source_target_pairs={{0,16},{16,0},{1,17},{17,1},{2,18},{18,2},{3,19},{19,3},{4,20},{20... | collective-permute-start | bytes 3145736 | tf_op jit(solution)/shard_map/ppermute | solution.py:15
  94.5 4.1 %collective-permute-start.13 = (f32[1,128,16,128]{3,1,2,0:T(8,128)S(1)}, f32[1,128,16,128]{3,1,2,0:T(8,128)S(1)}, u32[]{:S(2)}, u32[]{:S(2)}) collective-permute-start(f32[1,128,16,128]{3,1,2,0:T(8,128)S(1)} %get-tuple-element.28), channel_id=1, source_target_pairs={{16,0},{0,16},{17,1},{1,17},{18,2},{2,18},{19,3},{3,19},{20,4},{4,... | collective-permute-start | bytes 3145736 | tf_op jit(solution)/shard_map/ppermute | solution.py:18
  98.7 4.4 %collective-permute-start.14 = (f32[6,1,16,128]{3,1,2,0:T(1,128)S(1)}, f32[6,1,16,128]{3,1,2,0:T(1,128)S(1)}, u32[]{:S(2)}, u32[]{:S(2)}) collective-permute-start(f32[6,1,16,128]{3,1,2,0:T(1,128)S(1)} %get-tuple-element.19), channel_id=1, source_target_pairs={{0,8},{8,0},{1,9},{9,1},{2,10},{10,2},{3,11},{11,3},{4,12},{12,4},... | collective-permute-start | bytes 147464 | tf_op jit(solution)/shard_map/ppermute | solution.py:15
  99.5 4.1 %collective-permute-start.15 = (f32[6,1,16,128]{3,1,2,0:T(1,128)S(1)}, f32[6,1,16,128]{3,1,2,0:T(1,128)S(1)}, u32[]{:S(2)}, u32[]{:S(2)}) collective-permute-start(f32[6,1,16,128]{3,1,2,0:T(1,128)S(1)} %get-tuple-element.20), channel_id=1, source_target_pairs={{8,0},{0,8},{9,1},{1,9},{10,2},{2,10},{11,3},{3,11},{12,4},{4,12},... | collective-permute-start | bytes 147464 | tf_op jit(solution)/shard_map/ppermute | solution.py:18
  103.7 12.6 %collective-permute-start.16 = (f32[6,130,1,128]{3,1,2,0:T(8,128)S(1)}, f32[6,130,1,128]{3,1,2,0:T(8,128)S(1)}, u32[]{:S(2)}, u32[]{:S(2)}) collective-permute-start(f32[6,130,1,128]{3,1,2,0:T(8,128)S(1)} %get-tuple-element.11), channel_id=1, source_target_pairs={{0,4},{4,0},{1,5},{5,1},{2,6},{6,2},{3,7},{7,3},{8,12},{12,8},{9,1... | collective-permute-start | bytes 1198088 | tf_op jit(solution)/shard_map/ppermute | solution.py:15
  105.5 18.0 %collective-permute-start.17 = (f32[6,130,1,128]{3,1,2,0:T(8,128)S(1)}, f32[6,130,1,128]{3,1,2,0:T(8,128)S(1)}, u32[]{:S(2)}, u32[]{:S(2)}) collective-permute-start(f32[6,130,1,128]{3,1,2,0:T(8,128)S(1)} %get-tuple-element.12), channel_id=1, source_target_pairs={{4,0},{0,4},{5,1},{1,5},{6,2},{2,6},{7,3},{3,7},{12,8},{8,12},{13,... | collective-permute-start | bytes 1198088 | tf_op jit(solution)/shard_map/ppermute | solution.py:18
  131.7 2.7 %collective-permute-start.18 = (f32[1,128,16,128]{3,1,2,0:T(8,128)S(1)}, f32[1,128,16,128]{3,1,2,0:T(8,128)S(1)}, u32[]{:S(2)}, u32[]{:S(2)}) collective-permute-start(f32[1,128,16,128]{3,1,2,0:T(8,128)S(1)} %get-tuple-element.25), channel_id=1, source_target_pairs={{0,16},{16,0},{1,17},{17,1},{2,18},{18,2},{3,19},{19,3},{4,20},{20... | collective-permute-start | bytes 3145736 | tf_op jit(solution)/shard_map/ppermute | solution.py:15
  131.8 4.1 %collective-permute-start.19 = (f32[1,128,16,128]{3,1,2,0:T(8,128)S(1)}, f32[1,128,16,128]{3,1,2,0:T(8,128)S(1)}, u32[]{:S(2)}, u32[]{:S(2)}) collective-permute-start(f32[1,128,16,128]{3,1,2,0:T(8,128)S(1)} %get-tuple-element.26), channel_id=1, source_target_pairs={{16,0},{0,16},{17,1},{1,17},{18,2},{2,18},{19,3},{3,19},{20,4},{4,... | collective-permute-start | bytes 3145736 | tf_op jit(solution)/shard_map/ppermute | solution.py:18
  136.0 4.6 %collective-permute-start.20 = (f32[6,1,16,128]{3,1,2,0:T(1,128)S(1)}, f32[6,1,16,128]{3,1,2,0:T(1,128)S(1)}, u32[]{:S(2)}, u32[]{:S(2)}) collective-permute-start(f32[6,1,16,128]{3,1,2,0:T(1,128)S(1)} %get-tuple-element.17), channel_id=1, source_target_pairs={{0,8},{8,0},{1,9},{9,1},{2,10},{10,2},{3,11},{11,3},{4,12},{12,4},... | collective-permute-start | bytes 147464 | tf_op jit(solution)/shard_map/ppermute | solution.py:15
  137.3 4.1 %collective-permute-start.21 = (f32[6,1,16,128]{3,1,2,0:T(1,128)S(1)}, f32[6,1,16,128]{3,1,2,0:T(1,128)S(1)}, u32[]{:S(2)}, u32[]{:S(2)}) collective-permute-start(f32[6,1,16,128]{3,1,2,0:T(1,128)S(1)} %get-tuple-element.18), channel_id=1, source_target_pairs={{8,0},{0,8},{9,1},{1,9},{10,2},{2,10},{11,3},{3,11},{12,4},{4,12},... | collective-permute-start | bytes 147464 | tf_op jit(solution)/shard_map/ppermute | solution.py:18
  141.5 12.6 %collective-permute-start.22 = (f32[6,130,1,128]{3,1,2,0:T(8,128)S(1)}, f32[6,130,1,128]{3,1,2,0:T(8,128)S(1)}, u32[]{:S(2)}, u32[]{:S(2)}) collective-permute-start(f32[6,130,1,128]{3,1,2,0:T(8,128)S(1)} %get-tuple-element.9), channel_id=1, source_target_pairs={{0,4},{4,0},{1,5},{5,1},{2,6},{6,2},{3,7},{7,3},{8,12},{12,8},{9,1... | collective-permute-start | bytes 1198088 | tf_op jit(solution)/shard_map/ppermute | solution.py:15
  143.2 18.3 %collective-permute-start.23 = (f32[6,130,1,128]{3,1,2,0:T(8,128)S(1)}, f32[6,130,1,128]{3,1,2,0:T(8,128)S(1)}, u32[]{:S(2)}, u32[]{:S(2)}) collective-permute-start(f32[6,130,1,128]{3,1,2,0:T(8,128)S(1)} %get-tuple-element.10), channel_id=1, source_target_pairs={{4,0},{0,4},{5,1},{1,5},{6,2},{2,6},{7,3},{3,7},{12,8},{8,12},{13,... | collective-permute-start | bytes 1198088 | tf_op jit(solution)/shard_map/ppermute | solution.py:18
Sparse Core Ops, SparseCore 0:
  171.8 29.3 all-reduce.2
where the time goes:
time: 217 us
  waiting for transfers between devices  118 us (54%)
  other arithmetic  45.2 us (21%)
  starting transfers between devices  20.2 us (9%)
  local copies, waits for them, and re-layouts  18.7 us (9%)
  between operations  14.2 us (7%)
    ppermute x12, waiting for transfers between devices, extended(): lax.ppermute(lax.slice_in_dim(block, block.shape[dim] - width, None, axis...  58.4 us
    ppermute x12, waiting for transfers between devices, extended(): lax.ppermute(lax.slice_in_dim(block, 0, width, axis=dim), axis, backward)  37.1 us
    add x3, other arithmetic, one_step(): return middle + diffusivity * spread + source  30.4 us
    psum x1, waiting for transfers between devices, on_device(): lax.psum((jnp.sum(moved, axis=2, keepdims=True), jnp.sum(moved * moved, a...  22.9 us
    unnamed x15, local copies, waits for them, and re-layouts  17.7 us
    ppermute x12, starting transfers between devices, extended(): lax.ppermute(lax.slice_in_dim(block, block.shape[dim] - width, None, axis...  13.3 us
    reduce_sum x1, other arithmetic, on_device(): jnp.sum(moved, axis=2, keepdims=True)  10.2 us
    ppermute x12, starting transfers between devices, extended(): lax.ppermute(lax.slice_in_dim(block, 0, width, axis=dim), axis, backward)  6.81 us
  transfers between devices with their start and end apart: 25, of which 24 were waited for; matrix products, arithmetic and copies ran while one was open for 4% of the time, Pallas kernels for 0%

commit v1 on v0

v1 whole, which is shorter than its diff:
```python
import functools

import jax
import jax.numpy as jnp
from jax import lax
from jax.experimental import pallas as pl
from jax.experimental.pallas import tpu as pltpu
from jax.sharding import PartitionSpec as P

STEPS = 4
PAD = 8
EPSILON = 0.0001
MESH = pl.DeviceIdType.MESH


def rows_of(extent):
    for rows in (32, 16, 8):
        if extent % rows == 0:
            return rows
    return extent


def steps_kernel(
    sizes, shape, tracer, diffusivity, source, last, stats,
    field, coeff, forcing, own, others,
    load_sem, lev_send, lev_recv, lat_send, lat_recv, lon_send, lon_recv, stat_send, stat_recv,
):
    n_j, n_i, n_k, _ = shape
    n_lat, n_lon, n_lev = sizes
    inner = pl.ds(PAD, n_i)
    whole_j = pl.ds(1, n_j)
    chunk = rows_of(n_i)
    lat, lon, lev = lax.axis_index("lat"), lax.axis_index("lon"), lax.axis_index("lev")
    lat_up, lat_down = lax.rem(lat + 1, n_lat), lax.rem(lat + n_lat - 1, n_lat)
    lon_up, lon_down = lax.rem(lon + 1, n_lon), lax.rem(lon + n_lon - 1, n_lon)
    lev_up, lev_down = lax.rem(lev + 1, n_lev), lax.rem(lev + n_lev - 1, n_lev)

    def load(which, k):
        array = (tracer, diffusivity, source)[which]
        if which == 0:
            target = field.at[0, k + 1, whole_j, inner, :]
        else:
            target = (coeff, forcing)[which - 1].at[k]
        return pltpu.make_async_copy(array.at[:, :, k, :], target, load_sem.at[which, k])

    def remote(src, dst, send, recv, device):
        return pltpu.make_async_remote_copy(
            src_ref=src, dst_ref=dst, send_sem=send, recv_sem=recv,
            device_id=device, device_id_type=MESH,
        )

    def lev_copies(step, j):
        down = remote(
            field.at[step, 1, j, inner, :], field.at[step, n_k + 1, j, inner, :],
            lev_send.at[step, j - 1, 0], lev_recv.at[step, j - 1, 0], {"lev": lev_down},
        )
        up = remote(
            field.at[step, n_k, j, inner, :], field.at[step, 0, j, inner, :],
            lev_send.at[step, j - 1, 1], lev_recv.at[step, j - 1, 1], {"lev": lev_up},
        )
        return down, up

    parts = (pl.ds(1, 1), pl.ds(n_k, 1), pl.ds(2, n_k - 2))

    def lat_copy(step, part, side):
        k = parts[part]
        src, dst, to = ((1, n_j + 1, lat_down), (n_j, 0, lat_up))[side]
        return remote(
            field.at[step, k, src, inner, :], field.at[step, k, dst, inner, :],
            lat_send.at[step, part, side], lat_recv.at[step, part, side], {"lat": to},
        )

    def lon_copy(step, part, side):
        k = parts[part]
        src, dst, to = (
            (PAD, PAD + n_i, lon_down), (PAD + n_i - 1, PAD - 1, lon_up)
        )[side]
        return remote(
            field.at[step, k, whole_j, pl.ds(src, 1), :],
            field.at[step, k, whole_j, pl.ds(dst, 1), :],
            lon_send.at[step, part, side], lon_recv.at[step, part, side], {"lon": to},
        )

    def stat_copies(j):
        return [
            remote(
                own.at[j - 1], others.at[n_lev - 1 - away, j - 1],
                stat_send.at[away - 1, j - 1], stat_recv.at[n_lev - 1 - away, j - 1],
                {"lev": lax.rem(lev + away, n_lev)},
            )
            for away in range(1, n_lev)
        ]

    def update(step, k, j):
        for low in range(0, n_i, chunk):
            r = PAD + low
            middle = field[step, k, j, pl.ds(r, chunk), :]
            spread = (
                field[step, k, j - 1, pl.ds(r, chunk), :] + field[step, k, j + 1, pl.ds(r, chunk), :]
                + field[step, k, j, pl.ds(r - 1, chunk), :] + field[step, k, j, pl.ds(r + 1, chunk), :]
                + field[step, k - 1, j, pl.ds(r, chunk), :] + field[step, k + 1, j, pl.ds(r, chunk), :]
                - 6.0 * middle
            )
            rows = pl.ds(low, chunk)
            value = middle + coeff[k - 1, j - 1, rows, :] * spread + forcing[k - 1, j - 1, rows, :]
            if step == STEPS - 1:
                last[k - 1, j - 1, rows, :] = value
            else:
                field[step + 1, k, j, pl.ds(r, chunk), :] = value

    def summarise(j):
        for low in range(0, n_i, chunk):
            rows = pl.ds(low, chunk)
            total = last[0, j - 1, rows, :]
            for k in range(1, n_k):
                total = total + last[k, j - 1, rows, :]
            mean = total * (1.0 / n_k)
            squares = jnp.zeros_like(mean)
            for k in range(n_k):
                moved = last[k, j - 1, rows, :] - mean
                squares = squares + moved * moved
            own[j - 1, 0, rows, :] = mean
            own[j - 1, 1, rows, :] = squares

    def combine(j):
        for low in range(0, n_i, chunk):
            rows = pl.ds(low, chunk)
            means = [own[j - 1, 0, rows, :]] + [others[p, j - 1, 0, rows, :] for p in range(n_lev - 1)]
            mean = functools.reduce(jnp.add, means) * (1.0 / n_lev)
            squares = own[j - 1, 1, rows, :]
            for p in range(n_lev - 1):
                squares = squares + others[p, j - 1, 1, rows, :]
            for part in means:
                squares = squares + n_k * ((part - mean) * (part - mean))
            stats[j - 1, 0, rows, :] = mean
            stats[j - 1, 1, rows, :] = lax.rsqrt(squares * (1.0 / (n_k * n_lev)) + EPSILON)

    def over_k(first, end, body):
        def wrapped(k, carry):
            body(k)
            return carry
        lax.fori_loop(first, end, wrapped, 0)

    edges = (0, n_k - 1)
    for k in (0, n_k - 1, 1, n_k - 2):
        load(0, k).start()
    for which in (1, 2):
        for k in edges:
            load(which, k).start()
    over_k(2, n_k - 2, lambda k: load(0, k).start())
    for which in (1, 2):
        over_k(1, n_k - 1, lambda k: load(which, k).start())

    barrier = pltpu.get_barrier_semaphore()
    greeted = (
        [{"lat": lax.rem(lat + a, n_lat)} for a in sorted({1, n_lat - 1})]
        + [{"lon": lax.rem(lon + a, n_lon)} for a in sorted({1, n_lon - 1})]
        + [{"lev": lax.rem(lev + a, n_lev)} for a in range(1, n_lev)]
    )
    for device in greeted:
        pl.semaphore_signal(barrier, inc=1, device_id=device, device_id_type=MESH)
    pl.semaphore_wait(barrier, len(greeted))

    for k in edges:
        load(0, k).wait()
    for j in range(1, n_j + 1):
        for copy in lev_copies(0, j):
            copy.start()
    for part in (0, 1):
        for side in (0, 1):
            lat_copy(0, part, side).start()
            lon_copy(0, part, side).start()
    for k in (1, n_k - 2):
        load(0, k).wait()
    for which in (1, 2):
        for k in edges:
            load(which, k).wait()

    def inside(step):
        for side in (0, 1):
            lat_copy(step, 2, side).wait_recv()
            lon_copy(step, 2, side).wait_recv()

        def body(k):
            def across(j, carry):
                update(step, k, j)
                return carry
            lax.fori_loop(1, n_j + 1, across, 0)

        over_k(2, n_k, body)
        if step < STEPS - 1:
            for side in (0, 1):
                lat_copy(step + 1, 2, side).start()
                lon_copy(step + 1, 2, side).start()

    def outside(step):
        for part in (0, 1):
            for side in (0, 1):
                lat_copy(step, part, side).wait_recv()
                lon_copy(step, part, side).wait_recv()
        for j in range(1, n_j + 1):
            for copy in lev_copies(step, j):
                copy.wait_recv()
            update(step, 1, j)
            update(step, n_k, j)
            if step < STEPS - 1:
                for copy in lev_copies(step + 1, j):
                    copy.start()
                for side, edge in ((0, 1), (1, n_j)):
                    if j == edge:
                        for part in (0, 1):
                            lat_copy(step + 1, part, side).start()
            else:
                summarise(j)
                for copy in stat_copies(j):
                    copy.start()
        if step < STEPS - 1:
            for part in (0, 1):
                for side in (0, 1):
                    lon_copy(step + 1, part, side).start()

    over_k(2, n_k - 2, lambda k: load(0, k).wait())
    for side in (0, 1):
        lat_copy(0, 2, side).start()
        lon_copy(0, 2, side).start()
    outside(0)
    for which in (1, 2):
        over_k(1, n_k - 1, lambda k: load(which, k).wait())
    inside(0)
    for step in range(1, STEPS):
        inside(step)
        outside(step)
    for j in range(1, n_j + 1):
        for copy in stat_copies(j):
            copy.wait_recv()
        combine(j)

    for step in range(STEPS):
        for j in range(1, n_j + 1):
            for copy in lev_copies(step, j):
                copy.wait_send()
        for part in range(3):
            for side in (0, 1):
                lat_copy(step, part, side).wait_send()
                lon_copy(step, part, side).wait_send()
    for j in range(1, n_j + 1):
        for copy in stat_copies(j):
            copy.wait_send()


def finish_kernel(n_k, rows, last, stats, standardized, tracer_end):
    j, block = pl.program_id(0), pl.program_id(1)
    for low in range(0, rows, 8):
        here = pl.ds(pl.multiple_of(block * rows + low, 8), 8)
        mean = stats[j, 0, here, :]
        scale = stats[j, 1, here, :]
        for k in range(n_k):
            value = last[k, j, here, :]
            place = pl.ds(low * n_k + k, 8, stride=n_k)
            tracer_end[0, place, :] = value
            standardized[0, place, :] = (value - mean) * scale


def on_device(sizes, tracer, diffusivity, source):
    shape = tracer.shape
    n_j, n_i, n_k, levels = shape
    n_lev = sizes[2]
    f32 = jnp.float32
    sem = pltpu.SemaphoreType.DMA
    last, stats = pl.pallas_call(
        functools.partial(steps_kernel, sizes, shape),
        out_shape=(
            pltpu.VMEM((n_k, n_j, n_i, levels), f32),
            pltpu.VMEM((n_j, 2, n_i, levels), f32),
        ),
        in_specs=[pl.BlockSpec(memory_space=pl.ANY)] * 3,
        out_specs=(pl.BlockSpec(memory_space=pltpu.VMEM),) * 2,
        scratch_shapes=[
            pltpu.VMEM((STEPS, n_k + 2, n_j + 2, n_i + 2 * PAD, levels), f32),
            pltpu.VMEM((n_k, n_j, n_i, levels), f32),
            pltpu.VMEM((n_k, n_j, n_i, levels), f32),
            pltpu.VMEM((n_j, 2, n_i, levels), f32),
            pltpu.VMEM((n_lev - 1, n_j, 2, n_i, levels), f32),
            sem((3, n_k)),
            sem((STEPS, n_j, 2)), sem((STEPS, n_j, 2)),
            sem((STEPS, 3, 2)), sem((STEPS, 3, 2)),
            sem((STEPS, 3, 2)), sem((STEPS, 3, 2)),
            sem((n_lev - 1, n_j)), sem((n_lev - 1, n_j)),
        ],
        compiler_params=pltpu.CompilerParams(
            collective_id=0, has_side_effects=True, vmem_limit_bytes=48 * 1024 * 1024,
        ),
    )(tracer, diffusivity, source)
    rows = rows_of(n_i)
    block = pl.BlockSpec((1, rows * n_k, levels), lambda j, i: (j, i, 0))
    whole = pl.BlockSpec(memory_space=pltpu.VMEM)
    flat = jax.ShapeDtypeStruct((n_j, n_i * n_k, levels), f32)
    standardized, tracer_end = pl.pallas_call(
        functools.partial(finish_kernel, n_k, rows),
        grid=(n_j, n_i // rows),
        out_shape=(flat, flat),
        in_specs=[whole, whole],
        out_specs=(block, block),
        compiler_params=pltpu.CompilerParams(vmem_limit_bytes=24 * 1024 * 1024),
    )(last, stats)
    return standardized.reshape(shape), tracer_end.reshape(shape)


def solution(mesh):
    sizes = (mesh.shape["lat"], mesh.shape["lon"], mesh.shape["lev"])
    spec = P(("unit", "lat"), "lon", "lev", None)
    return jax.shard_map(
        functools.partial(on_device, sizes),
        mesh=mesh,
        in_specs=(spec, spec, spec),
        out_specs=(spec, spec),
        check_vma=False,
    )
```

time: 217 us -> 72.8 us (0.34)
  waiting for transfers between devices: 118 us -> 0 us
  Pallas kernels: 0 us -> 72.1 us
  other arithmetic: 45.2 us -> 0 us
  starting transfers between devices: 20.2 us -> 0 us
  local copies, waits for them, and re-layouts: 18.7 us -> 0 us
  between operations: 14.2 us -> 0.64 us
    ppermute x24 -> x0, waiting for transfers between devices: 95.4 us -> none  [the longest x12 58.4 us: extended(): lax.ppermute(lax.slice_in_dim(block, block.shape[dim] - width, None, axis...]
    pallas_call x0 -> x2, Pallas kernels: none -> 72.1 us  [the longest x1 64.6 us: on_device(): pl.pallas_call(functools.partial(steps_kernel, sizes, shape), out_shape=(...]
    add x3 -> x0, other arithmetic: 30.4 us -> none  [one_step(): return middle + diffusivity * spread + source]
    psum x1 -> x0, waiting for transfers between devices: 22.9 us -> none  [on_device(): lax.psum((jnp.sum(moved, axis=2, keepdims=True), jnp.sum(moved * moved, a...]
    ppermute x24 -> x0, starting transfers between devices: 20.1 us -> none  [the longest x12 13.3 us: extended(): lax.ppermute(lax.slice_in_dim(block, block.shape[dim] - width, None, axis...]
    unnamed x15 -> x0, local copies, waits for them, and re-layouts: 17.7 us -> none
    reduce_sum x1 -> x0, other arithmetic: 10.2 us -> none  [on_device(): jnp.sum(moved, axis=2, keepdims=True)]
    mul x1 -> x0, other arithmetic: 2.99 us -> none  [on_device(): standardized = centred * lax.rsqrt(line_variance + 0.0001)]
  transfers between devices with their start and end apart: 25 -> 0, of which waited for: 24 -> 0; matrix products, arithmetic and copies ran while one was open for 4% -> 0% of each run, Pallas kernels for 0% -> 0%
where the time goes in v1:
time: 72.8 us; the launch traced here: 72.7 us
  Pallas kernels  72.1 us (99%)
    pallas_call x1, Pallas kernels, on_device(): pl.pallas_call(functools.partial(steps_kernel, sizes, shape), out_shape=(...  64.6 us
    pallas_call x1, Pallas kernels, on_device(): pl.pallas_call(functools.partial(finish_kernel, n_k, rows), grid=(n_j, n_...  7.4 us

profile of v1, /device:TPU:0, one launch (start us, length us, event | category | flops | bytes accessed | tf_op | source)
XLA Modules:
  0.0 72.7 jit_solution(11969313920248262689)
XLA Ops:
  0.6 64.6 %shard_map.50 = (f32[16,4,128,128]{3,2,1,0:T(8,128)S(1)}, f32[4,2,128,128]{3,2,1,0:T(8,128)S(1)}) custom-call(f32[4,128,16,128]{3,2,1,0:T(8,128)} %tracer.1, f32[4,128,16,128]{3,2,1,0:T(8,128)} %diffusivity.1, f32[4,128,16,128]{3,2,1,0:T(8,128)} %source.1), custom_call_target="tpu_custom_call" | custom-call | tf_op jit(solution)/shard_map/pallas_call | solution.py:270
  65.3 7.4 %shard_map.51 = (f32[4,2048,128]{2,1,0:T(8,128)}, f32[4,2048,128]{2,1,0:T(8,128)}) custom-call(f32[16,4,128,128]{3,2,1,0:T(8,128)S(1)} %get-tuple-element.6.last, f32[4,2,128,128]{3,2,1,0:T(8,128)S(1)} %get-tuple-element.7.stats), custom_call_target="tpu_custom_call" | custom-call | tf_op jit(solution)/shard_map/pallas_call | solution.py:298

commit v2 on v1

--- a/solution.py
+++ b/solution.py
@@ -21,8 +21,8 @@
 
 
 def steps_kernel(
-    sizes, shape, tracer, diffusivity, source, last, stats,
-    field, coeff, forcing, own, others,
+    sizes, shape, tracer, diffusivity, source, standardized, tracer_end,
+    field, coeff, forcing, last, own, others,
     load_sem, lev_send, lev_recv, lat_send, lat_recv, lon_send, lon_recv, stat_send, stat_recv,
 ):
     n_j, n_i, n_k, _ = shape
@@ -105,6 +105,8 @@
             value = middle + coeff[k - 1, j - 1, rows, :] * spread + forcing[k - 1, j - 1, rows, :]
             if step == STEPS - 1:
                 last[k - 1, j - 1, rows, :] = value
+                place = pl.ds(low * n_k + k - 1, chunk, stride=n_k)
+                tracer_end[j - 1, place, :] = value
             else:
                 field[step + 1, k, j, pl.ds(r, chunk), :] = value
 
@@ -132,8 +134,10 @@
                 squares = squares + others[p, j - 1, 1, rows, :]
             for part in means:
                 squares = squares + n_k * ((part - mean) * (part - mean))
-            stats[j - 1, 0, rows, :] = mean
-            stats[j - 1, 1, rows, :] = lax.rsqrt(squares * (1.0 / (n_k * n_lev)) + EPSILON)
+            scale = lax.rsqrt(squares * (1.0 / (n_k * n_lev)) + EPSILON)
+            for k in range(n_k):
+                place = pl.ds(low * n_k + k, chunk, stride=n_k)
+                standardized[j - 1, place, :] = (last[k, j - 1, rows, :] - mean) * scale
 
     def over_k(first, end, body):
         def wrapped(k, carry):
@@ -248,17 +252,16 @@
             copy.wait_send()
 
 
-def finish_kernel(n_k, rows, last, stats, standardized, tracer_end):
-    j, block = pl.program_id(0), pl.program_id(1)
-    for low in range(0, rows, 8):
-        here = pl.ds(pl.multiple_of(block * rows + low, 8), 8)
-        mean = stats[j, 0, here, :]
-        scale = stats[j, 1, here, :]
-        for k in range(n_k):
-            value = last[k, j, here, :]
-            place = pl.ds(low * n_k + k, 8, stride=n_k)
-            tracer_end[0, place, :] = value
-            standardized[0, place, :] = (value - mean) * scale
+def write_kernel(first, second, first_out, second_out, sem):
+    copies = [
+        pltpu.make_async_copy(src.at[j], dst.at[j], sem.at[which, j])
+        for j in range(first.shape[0])
+        for which, (src, dst) in enumerate(((first, first_out), (second, second_out)))
+    ]
+    for copy in copies:
+        copy.start()
+    for copy in copies:
+        copy.wait()
 
 
 def on_device(sizes, tracer, diffusivity, source):
@@ -267,16 +270,17 @@
     n_lev = sizes[2]
     f32 = jnp.float32
     sem = pltpu.SemaphoreType.DMA
-    last, stats = pl.pallas_call(
+    standardized, tracer_end = pl.pallas_call(
         functools.partial(steps_kernel, sizes, shape),
         out_shape=(
-            pltpu.VMEM((n_k, n_j, n_i, levels), f32),
-            pltpu.VMEM((n_j, 2, n_i, levels), f32),
+            pltpu.VMEM((n_j, n_i * n_k, levels), f32),
+            pltpu.VMEM((n_j, n_i * n_k, levels), f32),
         ),
         in_specs=[pl.BlockSpec(memory_space=pl.ANY)] * 3,
         out_specs=(pl.BlockSpec(memory_space=pltpu.VMEM),) * 2,
         scratch_shapes=[
             pltpu.VMEM((STEPS, n_k + 2, n_j + 2, n_i + 2 * PAD, levels), f32),
+            pltpu.VMEM((n_k, n_j, n_i, levels), f32),
             pltpu.VMEM((n_k, n_j, n_i, levels), f32),
             pltpu.VMEM((n_k, n_j, n_i, levels), f32),
             pltpu.VMEM((n_j, 2, n_i, levels), f32),
@@ -291,18 +295,15 @@
             collective_id=0, has_side_effects=True, vmem_limit_bytes=48 * 1024 * 1024,
         ),
     )(tracer, diffusivity, source)
-    rows = rows_of(n_i)
-    block = pl.BlockSpec((1, rows * n_k, levels), lambda j, i: (j, i, 0))
-    whole = pl.BlockSpec(memory_space=pltpu.VMEM)
     flat = jax.ShapeDtypeStruct((n_j, n_i * n_k, levels), f32)
     standardized, tracer_end = pl.pallas_call(
-        functools.partial(finish_kernel, n_k, rows),
-        grid=(n_j, n_i // rows),
+        write_kernel,
         out_shape=(flat, flat),
-        in_specs=[whole, whole],
-        out_specs=(block, block),
-        compiler_params=pltpu.CompilerParams(vmem_limit_bytes=24 * 1024 * 1024),
-    )(last, stats)
+        in_specs=[pl.BlockSpec(memory_space=pltpu.VMEM)] * 2,
+        out_specs=(pl.BlockSpec(memory_space=pl.ANY),) * 2,
+        scratch_shapes=[sem((2, n_j))],
+        compiler_params=pltpu.CompilerParams(vmem_limit_bytes=1024 * 1024),
+    )(standardized, tracer_end)
     return standardized.reshape(shape), tracer_end.reshape(shape)
 
 

time: 72.8 us -> 69.2 us (0.951)
  Pallas kernels: 72.1 us -> 68.4 us
    pallas_call x1, Pallas kernels: 7.4 us -> 3.37 us  [on_device(): pl.pallas_call(write_kernel, out_shape=(flat, flat), in_specs=[pl.BlockSp...]
where the time goes in v2:
time: 69.2 us; the launch traced here: 69 us
  Pallas kernels  68.4 us (99%)
    pallas_call x1, Pallas kernels, on_device(): pl.pallas_call(functools.partial(steps_kernel, sizes, shape), out_shape=(...  65 us
    pallas_call x1, Pallas kernels, on_device(): pl.pallas_call(write_kernel, out_shape=(flat, flat), in_specs=[pl.BlockSp...  3.37 us

profile of v2, /device:TPU:0, one launch (start us, length us, event | category | flops | bytes accessed | tf_op | source)
XLA Modules:
  0.0 69.0 jit_solution(3797698256036980981)
XLA Ops:
  0.6 65.0 %shard_map.50 = (f32[4,2048,128]{2,1,0:T(8,128)S(1)}, f32[4,2048,128]{2,1,0:T(8,128)S(1)}) custom-call(f32[4,128,16,128]{3,2,1,0:T(8,128)} %tracer.1, f32[4,128,16,128]{3,2,1,0:T(8,128)} %diffusivity.1, f32[4,128,16,128]{3,2,1,0:T(8,128)} %source.1), custom_call_target="tpu_custom_call" | custom-call | tf_op jit(solution)/shard_map/pallas_call | solution.py:273
  65.7 3.4 %shard_map.51 = (f32[4,2048,128]{2,1,0:T(8,128)}, f32[4,2048,128]{2,1,0:T(8,128)}) custom-call(f32[4,2048,128]{2,1,0:T(8,128)S(1)} %get-tuple-element.6.first, f32[4,2048,128]{2,1,0:T(8,128)S(1)} %get-tuple-element.7.second), custom_call_target="tpu_custom_call" | custom-call | tf_op jit(solution)/shard_map/pallas_call | solution.py:299
